TPU v7x, 32 devices: a whole 2x2x4 slice. The times are simulated.
32 devices in a mesh: gx: 4 (over y, core), gy: 2 (over x), gz: 4 (over z).
Axes of the slice: x: 2, y: 2, z: 4, core: 2. Of those that a mesh axis runs over, the one named last changes fastest.
Arguments:
- tokens: bfloat16 [32, 6144], P('gy'), may hold values from -6 to 6
- route: int32 [32, 2], P('gy'), may hold values from 0 to 3, all different within a row; in each aligned block of 16 rows (0 to 15, 16 to 31, ...) at most 12 rows name the same one
- weight_q: int32 [32, 2], P('gy'), may hold values from 1 to 65535
- w_gate: bfloat16 [4, 6144, 16384], P('gx', 'gy', 'gz'), may hold values from -0.078125 to 0.078125
- w_up: bfloat16 [4, 6144, 16384], P('gx', 'gy', 'gz'), may hold values from -0.078125 to 0.078125
- w_down: bfloat16 [4, 16384, 6144], P('gx', 'gz', 'gy'), may hold values from -0.046875 to 0.046875
Outputs:
- mixed: bfloat16 [32, 6144], P('gy', ('gx', 'gz'))
Inputs may be any that keep to these rules, and one draw needn't show every extreme that they name: `route`: the 2 entries of a row are different; in each block of 16 rows owned by one index of gy no expert is named by more than 12 rows, a bound that some block reaches.
All inputs are finite; a program needn't handle non-finite values.
Results may differ from a plain program's by a relative error of at most 0.0049.
Values may be sent and summed in bfloat16 or wider, within the bound.
A program may use at most 256 MiB of HBM per device.

v0:
```python
import jax
import jax.numpy as jnp
from jax import lax
from jax.sharding import PartitionSpec as P

CAP = 12


def per_device(tokens, route, weight_q, w_gate, w_up, w_down):
    expert = lax.axis_index("gx")
    width_z = lax.axis_size("gz")
    owners = lax.axis_size("gy")
    hits = (route == expert).astype(jnp.int32)
    routed = jnp.sum(hits, axis=1)
    slot_index = jnp.cumsum(routed) - 1
    columns = jnp.arange(CAP, dtype=jnp.int32)
    placing = (slot_index[None, :] == columns[:, None]) & (routed[None, :] > 0)
    place_half = placing.astype(jnp.bfloat16)
    place_full = placing.astype(jnp.float32)
    outgoing = jnp.dot(place_half, tokens, preferred_element_type=jnp.float32).astype(jnp.bfloat16)
    weights_f = weight_q.astype(jnp.float32)
    shares = weights_f / jnp.sum(weights_f, axis=1, keepdims=True)
    token_gate = jnp.sum(hits.astype(jnp.float32) * shares, axis=1)
    slot_gate = jnp.dot(place_full, token_gate, precision=lax.Precision.HIGHEST)
    depth = w_gate.shape[1]
    half = outgoing.reshape(CAP, owners, depth).transpose(1, 0, 2)
    piece = lax.all_to_all(half, "gy", split_axis=0, concat_axis=0, tiled=True)
    piece = piece.reshape(owners * CAP, depth)
    gate = jnp.dot(piece, w_gate[0], preferred_element_type=jnp.float32)
    upper = jnp.dot(piece, w_up[0], preferred_element_type=jnp.float32)
    both = lax.psum_scatter(jnp.stack([gate, upper]), "gy", scatter_dimension=2, tiled=True)
    hidden = (jax.nn.silu(both[0]) * both[1]).astype(jnp.bfloat16)
    down_local = w_down[0]
    partial_value = jnp.dot(
        lax.all_gather(hidden, "gy", axis=1, tiled=True),
        down_local,
        preferred_element_type=jnp.float32,
    )
    portion = CAP // width_z
    column_width = partial_value.shape[1]
    blocks = partial_value.reshape(owners, width_z, portion, column_width)
    narrowed = lax.psum_scatter(blocks, "gz", scatter_dimension=1, tiled=True)
    arrived = lax.all_to_all(narrowed, "gy", split_axis=0, concat_axis=1, tiled=True)
    full = jnp.transpose(arrived[0], (1, 0, 2)).reshape(portion, owners * column_width)
    first = lax.axis_index("gz") * portion
    gate_part = lax.dynamic_slice_in_dim(slot_gate, first, portion, 0)
    place_part = lax.dynamic_slice_in_dim(place_full, first, portion, 0)
    weighted = gate_part[:, None] * full
    contribution = jnp.dot(place_part.T, weighted, precision=lax.Precision.HIGHEST)
    result = lax.psum_scatter(contribution, ("gx", "gz"), scatter_dimension=1, tiled=True)
    return result.astype(jnp.bfloat16)


def solution(mesh):
    in_specs = (
        P("gy", None),
        P("gy", None),
        P("gy", None),
        P("gx", "gy", "gz"),
        P("gx", "gy", "gz"),
        P("gx", "gz", "gy"),
    )
    out_specs = P("gy", ("gx", "gz"))
    return jax.shard_map(
        per_device, mesh=mesh, in_specs=in_specs, out_specs=out_specs, check_vma=False
    )
```

profile of v0, /device:TPU:0, one launch (start us, length us, event | category | flops | bytes accessed | tf_op | source)
XLA Modules:
  0.0 181.3 jit_solution(7835118890817340249)
XLA Ops:
  6.5 0.7 fusion.21
  7.3 0.1 copy.23
  7.4 0.1 add_reduce_fusion
  7.5 0.2 convolution_convert_fusion
  7.7 0.1 reshape.49
  7.9 8.9 %all_to_all.14 = bf16[2,12,3072]{2,1,0:T(8,128)(2,1)S(1)} all-to-all(bf16[2,12,3072]{2,1,0:T(8,128)(2,1)S(1)} %bitcast.51), channel_id=1, replica_groups=mesh['gx'=4,'gy'=2,'gz'=4] {'gy'}, dimensions={0} | all-to-all | bytes 294912 | tf_op jit(solution)/shard_map/all_to_all | solution.py:27
  16.8 9.9 %fusion.6 = f32[1,24,4096]{2,1,0:T(8,128)S(1)} fusion(bf16[24,3072]{1,0:T(8,128)(2,1)S(1)} %reshape.50, bf16[1,3072,4096]{2,1,0:T(8,128)(2,1)} %param.9), kind=kOutput, calls=%fused_computation.7 | convolution fusion | flops 603979776 | bytes 25706496 | tf_op jit(solution)/shard_map/dot_general | solution.py:29
  26.7 10.0 %fusion.9 = f32[1,24,4096]{2,1,0:T(8,128)S(1)} fusion(bf16[24,3072]{1,0:T(8,128)(2,1)S(1)} %reshape.50, bf16[1,3072,4096]{2,1,0:T(8,128)(2,1)} %param.10), kind=kOutput, calls=%fused_computation.8 | convolution fusion | flops 603979776 | bytes 25706496 | tf_op jit(solution)/shard_map/dot_general | solution.py:30
  36.7 0.9 pad_maximum_fusion
  37.7 0.6 dynamic-slice
  38.3 17.3 %reduce-scatter.3.cloned.1.call-done = f32[2,24,2048]{2,1,0:T(8,128)} async-done(((f32[2,24,4096]{2,1,0:T(8,128)}), f32[2,24,2048]{2,1,0:T(8,128)}) %reduce-scatter.3.cloned.1.call-update) | async-done | bytes 393232 | tf_op jit(solution)/shard_map/reduce_scatter | solution.py:31
  55.6 1.1 fusion.13
  56.7 5.3 %all_gather.3 = bf16[24,4096]{1,0:T(8,128)(2,1)S(1)} all-gather(bf16[24,2048]{1,0:T(8,128)(2,1)S(1)} %fusion.13), channel_id=1, replica_groups=mesh['gx'=4,'gy'=2,'gz'=4] {'gy'}, dimensions={1}, use_global_device_ids=true | all-gather | bytes 294912 | tf_op jit(solution)/shard_map/all_gather | solution.py:35
  62.0 0.1 dot_general.24
  62.1 11.3 %fusion = f32[2,4,3,3072]{3,0,2,1:T(2,128)} fusion(bf16[1,4096,3072]{2,1,0:T(8,128)(2,1)} %param.11, bf16[2,4,3,4096]{3,2,1,0:T(4,128)(2,1)S(1)} %dot_general.24), kind=kOutput, calls=%fused_computation | convolution fusion | flops 603979776 | bytes 25657344 | tf_op jit(solution)/shard_map/dot_general | solution.py:34
  73.5 36.1 %all-reduce.3.cloned.1.call-done = f32[2,4,3,3072]{3,0,2,1:T(2,128)} async-done(((f32[2,4,3,3072]{3,0,2,1:T(2,128)}), f32[2,4,3,3072]{3,0,2,1:T(2,128)}) %all-reduce.3.cloned.1.call-update) | async-done | bytes 294928
  109.6 1.5 constant_dynamic-slice_fusion
  111.1 0.7 copy.27
  111.8 3.3 %all-to-all-start.1 = ((f32[2,1,3,3072]{3,1,2,0:T(1,128)}), f32[2,1,3,3072]{3,1,2,0:T(1,128)S(1)}, u32[]{:S(2)}, u32[]{:S(2)}) async-start(f32[2,1,3,3072]{3,1,2,0:T(1,128)} %copy.27), calls=%async_computation.2 | async-start | bytes 147456 | tf_op jit(solution)/shard_map/all_to_all | solution.py:43
  115.2 0.1 convolution_bitcast_fusion
  115.4 3.9 %all-to-all-done.1 = f32[2,1,3,3072]{3,1,2,0:T(1,128)S(1)} async-done(((f32[2,1,3,3072]{3,1,2,0:T(1,128)}), f32[2,1,3,3072]{3,1,2,0:T(1,128)S(1)}, u32[]{:S(2)}, u32[]{:S(2)}) %all-to-all-start.1) | async-done | bytes 73760 | tf_op jit(solution)/shard_map/all_to_all | solution.py:43
  119.4 1.2 fusion.15
  120.6 52.8 %reduce-scatter.5.cloned.1.call-done = f32[16,384]{1,0:T(8,128)} async-done(((f32[16,6144]{1,0:T(8,128)}), f32[16,384]{1,0:T(8,128)}) %reduce-scatter.5.cloned.1.call-update) | async-done | bytes 24592 | tf_op jit(solution)/shard_map/reduce_scatter | solution.py:50
  173.4 1.3 convert_element_type.25
  (26 shorter events, 0.5 us)
Async XLA Ops:
  6.5 1.0 copy-start
  6.5 49.1 %reduce-scatter.3.cloned.1.call-start = ((), (), s32[]{:S(2)}) async-start(), calls=%async_computation.4 | async-start | bytes 1179648 | tf_op jit(solution)/shard_map/reduce_scatter | solution.py:31
  26.7 11.0 %copy-start.4 = (u32[32]{0:T(128)S(1)}, u32[32]{0:T(128)}, u32[]{:S(2)}) copy-start(u32[32]{0:T(128)} %constant.30) | copy-start | bytes 388
  26.7 11.6 %copy-start.3 = (s32[16,2]{0,1:T(2,128)S(1)}, s32[16,2]{0,1:T(2,128)}, u32[]{:S(2)}) copy-start(s32[16,2]{0,1:T(2,128)} %param.8) | copy-start | bytes 388
  26.7 148.1 %copy-start.1 = (bf16[16,6144]{1,0:T(8,128)(2,1)S(1)}, bf16[16,6144]{1,0:T(8,128)(2,1)}, u32[]{:S(2)}) copy-start(bf16[16,6144]{1,0:T(8,128)(2,1)} %param.6) | copy-start | bytes 589828
  36.7 36.8 %copy-start.2 = (s32[16,2]{0,1:T(2,128)S(1)}, s32[16,2]{0,1:T(2,128)}, u32[]{:S(2)}) copy-start(s32[16,2]{0,1:T(2,128)} %param.7) | copy-start | bytes 388
  37.6 71.9 %all-reduce.3.cloned.1.call-start = ((), (), s32[]{:S(2)}) async-start(), calls=%async_computation.6 | async-start | bytes 589824
  111.8 7.5 %all-to-all-start.1 = ((f32[2,1,3,3072]{3,1,2,0:T(1,128)}), f32[2,1,3,3072]{3,1,2,0:T(1,128)S(1)}, u32[]{:S(2)}, u32[]{:S(2)}) async-start(f32[2,1,3,3072]{3,1,2,0:T(1,128)} %copy.27), calls=%async_computation.2 | async-start | bytes 147456 | tf_op jit(solution)/shard_map/all_to_all | solution.py:43
  115.1 58.3 %reduce-scatter.5.cloned.1.call-start = ((), (), s32[]{:S(2)}) async-start(), calls=%async_computation.5 | async-start | bytes 417792 | tf_op jit(solution)/shard_map/reduce_scatter | solution.py:50
Sparse Core Ops, SparseCore 0:
  37.8 17.8 reduce-scatter.2
  73.6 35.9 all-reduce.2
  120.7 52.6 reduce-scatter.4
where the time goes:
time: 182 us; the launch traced here: 181 us
  waiting for transfers between devices  110 us (60%)
  matrix products  32.7 us (18%)
  blocking collectives  14.1 us (8%)
  between operations  13.2 us (7%)
  other arithmetic  4.3 us (2%)
  starting transfers between devices  3.39 us (2%)
  local copies, waits for them, and re-layouts  3.36 us (2%)
    reduce_scatter x1, waiting for transfers between devices, per_device(): lax.psum_scatter(contribution, ('gx', 'gz'), scatter_dimension=1, tiled=T...  52.8 us
    unnamed x4, waiting for transfers between devices  36.1 us
    reduce_scatter x1, waiting for transfers between devices, per_device(): lax.psum_scatter(jnp.stack([gate, upper]), 'gy', scatter_dimension=2, til...  17.3 us
    dot_general x1, matrix products, per_device(): jnp.dot(lax.all_gather(hidden, 'gy', axis=1, tiled=True), down_local, pre...  11.3 us
    dot_general x1, matrix products, per_device(): upper = jnp.dot(piece, w_up[0], preferred_element_type=jnp.float32)  10 us
    dot_general x1, matrix products, per_device(): gate = jnp.dot(piece, w_gate[0], preferred_element_type=jnp.float32)  9.9 us
    all_to_all x1, blocking collectives, per_device(): piece = lax.all_to_all(half, 'gy', split_axis=0, concat_axis=0, tiled=True)  8.86 us
    all_gather x1, blocking collectives, per_device(): lax.all_gather(hidden, 'gy', axis=1, tiled=True)  5.29 us
  transfers between devices with their start and end apart: 4, of which 4 were waited for; matrix products, arithmetic and copies ran while one was open for 0% of the time, Pallas kernels for 0%

commit v1 on v0

--- a/solution.py
+++ b/solution.py
@@ -1,12 +1,22 @@
+import functools
+
 import jax
 import jax.numpy as jnp
 from jax import lax
+from jax.experimental import pallas as pl
+from jax.experimental.pallas import tpu as pltpu
 from jax.sharding import PartitionSpec as P
 
 CAP = 12
-
-
-def per_device(tokens, route, weight_q, w_gate, w_up, w_down):
+SLOTS = 16
+STEPS = 8
+RING = 5
+AHEAD = 4
+MESH = pl.DeviceIdType.MESH
+F32, BF16 = jnp.float32, jnp.bfloat16
+
+
+def plain(tokens, route, weight_q, w_gate, w_up, w_down):
     expert = lax.axis_index("gx")
     width_z = lax.axis_size("gz")
     owners = lax.axis_size("gy")
@@ -51,6 +61,287 @@
     return result.astype(jnp.bfloat16)
 
 
+def kernel(sizes, tok_hbm, route_hbm, wq_hbm, wg_hbm, wu_hbm, wd_hbm, out_ref,
+           tok, route, wq, gbuf, ubuf, dbuf_a, dbuf_b, xs, xsend, own, psend, precv,
+           hid, acc, sbuf, rbuf, sem_in, sem_g, sem_u, sem_a, sem_b,
+           tok_ss, tok_rs, ex_ss, ex_rs, out_ss, out_rs):
+    nx, ny, nz = sizes
+    gx, gy, gz = lax.axis_index("gx"), lax.axis_index("gy"), lax.axis_index("gz")
+    other = 1 - gy
+    depth, ffl = wg_hbm.shape[1], wg_hbm.shape[2]
+    cn = ffl // STEPS
+    half_steps = STEPS // 2
+    width = wd_hbm.shape[2]
+    nb = nx * nz // ny
+    bw = width // nb
+    token_rows = tok.shape[0]
+    kb = ffl // 2
+
+    def pair(j):
+        slot = lax.rem(j, RING)
+        cols = pl.ds(pl.multiple_of(j * cn, cn), cn)
+        return (pltpu.make_async_copy(wg_hbm.at[0, :, cols], gbuf.at[slot], sem_g.at[slot]),
+                pltpu.make_async_copy(wu_hbm.at[0, :, cols], ubuf.at[slot], sem_u.at[slot]))
+
+    def down_a(j):
+        rows = pl.ds(pl.multiple_of(j * cn, cn), cn)
+        return pltpu.make_async_copy(wd_hbm.at[0, rows, :], dbuf_a.at[j], sem_a.at[j])
+
+    low = gz < nz // 2
+
+    def block_of(i):
+        per = nb // nz
+        k = i // per
+        z = jnp.where(low, nz - 1 - k, k)
+        return lax.rem(i, per) * nz + z, lax.rem(i, per), z
+
+    def down_b(i):
+        b, _, _ = block_of(i)
+        cols = pl.ds(pl.multiple_of(b * bw, 128), bw)
+        return pltpu.make_async_copy(wd_hbm.at[0, kb:, cols], dbuf_b.at[i], sem_b.at[i])
+
+    ins = [pltpu.make_async_copy(tok_hbm, tok, sem_in.at[0]),
+           pltpu.make_async_copy(route_hbm, route, sem_in.at[1]),
+           pltpu.make_async_copy(wq_hbm, wq, sem_in.at[2])]
+    for c in ins:
+        c.start()
+    for j in range(AHEAD):
+        for c in pair(j):
+            c.start()
+
+    mine = gx * nz + gz
+    src_y = mine // nb
+    gx_first = gy * (nb // nz)
+    barrier = pltpu.get_barrier_semaphore()
+    pl.semaphore_signal(barrier, inc=1, device_id=(gx, other, gz), device_id_type=MESH)
+    for e in range(nx):
+        for z in range(nz):
+            @pl.when(jnp.logical_not((e == gx) & (src_y == gy) & (z == gz)))
+            def _():
+                pl.semaphore_signal(barrier, inc=1, device_id=(e, src_y, z), device_id_type=MESH)
+
+    for c in ins:
+        c.wait()
+
+    lane_t = lax.broadcasted_iota(jnp.int32, (token_rows, token_rows), 1)
+    sub_t = lax.broadcasted_iota(jnp.int32, (token_rows, token_rows), 0)
+    eye = (lane_t == sub_t).astype(F32)
+    upto = (lane_t <= sub_t).astype(F32)
+    r0, r1 = route[0:1, :], route[1:2, :]
+    w0, w1 = wq[0:1, :].astype(F32), wq[1:2, :].astype(F32)
+    total = w0 + w1
+    s0, s1 = w0 / total, w1 / total
+
+    def hit_row(e):
+        return ((r0 == e) | (r1 == e)).astype(F32)
+
+    hr = hit_row(gx)
+    hc = jnp.sum(eye * hr, axis=1, keepdims=True)
+    upper_tri = (sub_t <= lane_t).astype(F32)
+    slot_row = jnp.sum(upper_tri * hc, axis=0, keepdims=True) - 1.0
+    slots_sub = lax.broadcasted_iota(jnp.int32, (SLOTS, token_rows), 0).astype(F32)
+    place = ((slot_row == slots_sub) & (hr > 0.0)).astype(F32).astype(BF16)
+
+    spreads = []
+    slots_lane = lax.broadcasted_iota(jnp.int32, (token_rows, SLOTS), 1).astype(F32)
+    for e in range(nx):
+        h = hit_row(e)
+        g = jnp.where(r0 == e, s0, 0.0) + jnp.where(r1 == e, s1, 0.0)
+        slot_col = jnp.sum(upto * h, axis=1, keepdims=True) - 1.0
+        gate_col = jnp.sum(eye * g, axis=1, keepdims=True)
+        hit_col = jnp.sum(eye * h, axis=1, keepdims=True)
+        spreads.append(jnp.where((slot_col == slots_lane) & (hit_col > 0.0), gate_col, 0.0))
+
+    my_rows = pl.ds(pl.multiple_of(gy * SLOTS, SLOTS), SLOTS)
+    piece = depth // 3
+    for q in range(3):
+        theirs = pl.ds(pl.multiple_of(other * depth + q * piece, 128), piece)
+        xsend[:, q * piece:(q + 1) * piece] = jnp.dot(
+            place, tok[:, theirs], preferred_element_type=F32).astype(BF16)
+    for q in range(3):
+        ours = pl.ds(pl.multiple_of(gy * depth + q * piece, 128), piece)
+        xs[my_rows, q * piece:(q + 1) * piece] = jnp.dot(
+            place, tok[:, ours], preferred_element_type=F32).astype(BF16)
+
+    self_dest = src_y == gy
+    pl.semaphore_wait(barrier, ny * nb + 1 - self_dest.astype(jnp.int32))
+
+    partner = (gx, other, gz)
+    tok_copy = pltpu.make_async_remote_copy(
+        src_ref=xsend, dst_ref=xs.at[my_rows, :], send_sem=tok_ss, recv_sem=tok_rs,
+        device_id=partner, device_id_type=MESH)
+    tok_copy.start()
+    acc[...] = jnp.zeros_like(acc)
+    tok_copy.wait()
+
+    def exchange(j):
+        return pltpu.make_async_remote_copy(
+            src_ref=psend.at[j], dst_ref=precv.at[j], send_sem=ex_ss.at[j], recv_sem=ex_rs.at[j],
+            device_id=partner, device_id_type=MESH)
+
+    def project(j, carry):
+        slot = lax.rem(j, RING)
+        cg, cu = pair(j)
+
+        @pl.when(j + AHEAD < STEPS)
+        def _():
+            for c in pair(j + AHEAD):
+                c.start()
+
+        @pl.when((j + AHEAD >= STEPS) & (j + AHEAD < STEPS + half_steps // 2))
+        def _():
+            first = (j + AHEAD - STEPS) * 2
+            down_a(first).start()
+            down_a(first + 1).start()
+
+        @pl.when(j + AHEAD >= STEPS + half_steps // 2)
+        def _():
+            per = nb // (half_steps - half_steps // 2)
+            first = (j + AHEAD - STEPS - half_steps // 2) * per
+            for t in range(per):
+                down_b(first + t).start()
+
+        cg.wait()
+        g = jnp.dot(xs[...], gbuf[slot], preferred_element_type=F32)
+        own[j, 0] = g
+        psend[j, 0] = g.astype(BF16)
+        cu.wait()
+        u = jnp.dot(xs[...], ubuf[slot], preferred_element_type=F32)
+        own[j, 1] = u
+        psend[j, 1] = u.astype(BF16)
+        exchange(j).start()
+        return carry
+
+    lax.fori_loop(0, STEPS, project, 0)
+
+    def hidden(j):
+        exchange(j).wait_recv()
+        g = own[j, 0] + precv[j, 0].astype(F32)
+        u = own[j, 1] + precv[j, 1].astype(F32)
+        return (g * jax.nn.sigmoid(g) * u).astype(BF16)
+
+    nsub = 4
+    sw = width // nsub
+
+    def first_half(j, carry):
+        h = hidden(j)
+        down_a(j).wait()
+        for q in range(nsub):
+            cols = slice(q * sw, (q + 1) * sw)
+            acc[:, cols] += jnp.dot(h, dbuf_a[j, :, cols], preferred_element_type=F32)
+        return carry
+
+    lax.fori_loop(0, half_steps, first_half, 0)
+    for j in range(half_steps, STEPS):
+        hid[:, (j - half_steps) * cn:(j - half_steps + 1) * cn] = hidden(j)
+
+    def out_copy(i, o):
+        _, c, z = block_of(i)
+        here = gx * nz + gz
+        return pltpu.make_async_remote_copy(
+            src_ref=sbuf.at[i, o], dst_ref=rbuf.at[here], send_sem=out_ss.at[i, o],
+            recv_sem=out_rs.at[here], device_id=(gx_first + c, o, z), device_id_type=MESH)
+
+    def to_self(i, o):
+        _, c, z = block_of(i)
+        return (gx_first + c == gx) & (o == gy) & (z == gz)
+
+    def second_half(i, carry):
+        b, c, z = block_of(i)
+        cols = pl.ds(pl.multiple_of(b * bw, 128), bw)
+        down_b(i).wait()
+        y = acc[:, cols] + jnp.dot(hid[...], dbuf_b[i], preferred_element_type=F32)
+        yb = y.astype(BF16)
+        for o in range(ny):
+            part = yb[o * SLOTS:(o + 1) * SLOTS]
+            sbuf[i, o] = part
+
+            @pl.when(to_self(i, o))
+            def _():
+                rbuf[gx * nz + gz] = part
+
+            @pl.when(jnp.logical_not(to_self(i, o)))
+            def _():
+                out_copy(i, o).start()
+        return carry
+
+    lax.fori_loop(0, nb, second_half, 0)
+
+    sums = []
+    for e in range(nx):
+        s = None
+        for z in range(nz):
+            @pl.when(jnp.logical_not((e == gx) & (src_y == gy) & (z == gz)))
+            def _():
+                pltpu.make_async_remote_copy(
+                    src_ref=sbuf.at[0, 0], dst_ref=rbuf.at[e * nz + z], send_sem=out_ss.at[0, 0],
+                    recv_sem=out_rs.at[e * nz + z], device_id=(e, src_y, z),
+                    device_id_type=MESH).wait_recv()
+    for e in range(nx):
+        s = rbuf[e * nz].astype(F32)
+        for z in range(1, nz):
+            s = s + rbuf[e * nz + z].astype(F32)
+        sums.append(jnp.dot(spreads[e], s, precision=lax.Precision.HIGHEST,
+                            preferred_element_type=F32))
+    out_ref[...] = functools.reduce(lambda a, b: a + b, sums).astype(out_ref.dtype)
+
+    def drain(j, carry):
+        exchange(j).wait_send()
+        return carry
+
+    lax.fori_loop(0, STEPS, drain, 0)
+
+    def drain_out(i, carry):
+        for o in range(ny):
+            @pl.when(jnp.logical_not(to_self(i, o)))
+            def _():
+                out_copy(i, o).wait_send()
+        return carry
+
+    lax.fori_loop(0, nb, drain_out, 0)
+
+
+def fused(sizes, tokens, route, weight_q, w_gate, w_up, w_down):
+    nx, ny, nz = sizes
+    depth, ffl = w_gate.shape[1], w_gate.shape[2]
+    width = w_down.shape[2]
+    cn = ffl // STEPS
+    nb = nx * nz // ny
+    bw = width // nb
+    rows = ny * SLOTS
+    dma = pltpu.SemaphoreType.DMA
+    hbm = pl.BlockSpec(memory_space=pl.ANY)
+    return pl.pallas_call(
+        functools.partial(kernel, sizes),
+        out_shape=jax.ShapeDtypeStruct((tokens.shape[0], bw), BF16),
+        in_specs=[hbm] * 6,
+        out_specs=pl.BlockSpec(memory_space=pltpu.VMEM),
+        scratch_shapes=[
+            pltpu.VMEM(tokens.shape, BF16),
+            pltpu.VMEM(route.shape[::-1], jnp.int32),
+            pltpu.VMEM(route.shape[::-1], jnp.int32),
+            pltpu.VMEM((RING, depth, cn), BF16),
+            pltpu.VMEM((RING, depth, cn), BF16),
+            pltpu.VMEM((STEPS // 2, cn, width), BF16),
+            pltpu.VMEM((nb, ffl // 2, bw), BF16),
+            pltpu.VMEM((rows, depth), BF16),
+            pltpu.VMEM((SLOTS, depth), BF16),
+            pltpu.VMEM((STEPS, 2, rows, cn), F32),
+            pltpu.VMEM((STEPS, 2, rows, cn), BF16),
+            pltpu.VMEM((STEPS, 2, rows, cn), BF16),
+            pltpu.VMEM((rows, ffl // 2), BF16),
+            pltpu.VMEM((rows, width), F32),
+            pltpu.VMEM((nb, ny, SLOTS, bw), BF16),
+            pltpu.VMEM((nx * nz, SLOTS, bw), BF16),
+            dma((3,)), dma((RING,)), dma((RING,)), dma((STEPS // 2,)), dma((nb,)),
+            dma, dma, dma((STEPS,)), dma((STEPS,)), dma((nb, ny)), dma((nx * nz,)),
+        ],
+        compiler_params=pltpu.CompilerParams(
+            collective_id=0, has_side_effects=True, vmem_limit_bytes=67043328),
+        name="routed_ffn",
+    )(tokens, route.T, weight_q.T, w_gate, w_up, w_down)
+
+
 def solution(mesh):
     in_specs = (
         P("gy", None),
@@ -61,6 +352,8 @@
         P("gx", "gz", "gy"),
     )
     out_specs = P("gy", ("gx", "gz"))
+    sizes = tuple(mesh.shape[name] for name in ("gx", "gy", "gz"))
+    body = functools.partial(fused, sizes) if sizes[1] == 2 else plain
     return jax.shard_map(
-        per_device, mesh=mesh, in_specs=in_specs, out_specs=out_specs, check_vma=False
+        body, mesh=mesh, in_specs=in_specs, out_specs=out_specs, check_vma=False
     )

time: 182 us -> 36.9 us (0.20)
  waiting for transfers between devices: 110 us -> 0 us
  Pallas kernels: 0 us -> 35.4 us
  matrix products: 32.7 us -> 0 us
  blocking collectives: 14.1 us -> 0 us
  between operations: 13.2 us -> 0.01 us
  other arithmetic: 4.3 us -> 0 us
  starting transfers between devices: 3.39 us -> 0 us
  local copies, waits for them, and re-layouts: 3.36 us -> 1.31 us
    reduce_scatter x2 -> x0, waiting for transfers between devices: 70.2 us -> none  [the longest x1 52.8 us: per_device(): lax.psum_scatter(contribution, ('gx', 'gz'), scatter_dimension=1, tiled=T...]
    unnamed x4 -> x0, waiting for transfers between devices: 36.1 us -> none
    pallas_call x0 -> x1, Pallas kernels: none -> 35.4 us  [fused(): pl.pallas_call(functools.partial(kernel, sizes), out_shape=jax.ShapeDtype...]
    dot_general x6 -> x0, matrix products: 32.7 us -> none  [the longest x1 11.3 us: per_device(): jnp.dot(lax.all_gather(hidden, 'gy', axis=1, tiled=True), down_local, pre...]
    all_to_all x1 -> x0, blocking collectives: 8.86 us -> none  [per_device(): piece = lax.all_to_all(half, 'gy', split_axis=0, concat_axis=0, tiled=True)]
    all_gather x1 -> x0, blocking collectives: 5.29 us -> none  [per_device(): lax.all_gather(hidden, 'gy', axis=1, tiled=True)]
    all_to_all x1 -> x0, waiting for transfers between devices: 3.9 us -> none  [per_device(): lax.all_to_all(narrowed, 'gy', split_axis=0, concat_axis=1, tiled=True)]
    all_to_all x1 -> x0, starting transfers between devices: 3.31 us -> none  [per_device(): lax.all_to_all(narrowed, 'gy', split_axis=0, concat_axis=1, tiled=True)]
  transfers between devices with their start and end apart: 4 -> 0, of which waited for: 4 -> 0; matrix products, arithmetic and copies ran while one was open for 0% -> 0% of each run, Pallas kernels for 0% -> 0%
where the time goes in v1:
time: 36.9 us; the launch traced here: 36.7 us
  Pallas kernels  35.4 us (96%)
  local copies, waits for them, and re-layouts  1.31 us (4%)
    pallas_call x1, Pallas kernels, fused(): pl.pallas_call(functools.partial(kernel, sizes), out_shape=jax.ShapeDtype...  35.4 us
    unnamed x1, local copies, waits for them, and re-layouts  1.31 us

profile of v1, /device:TPU:0, one launch (start us, length us, event | category | flops | bytes accessed | tf_op | source)
XLA Modules:
  0.0 36.7 jit_solution(12119158886151181055)
XLA Ops:
  0.0 35.4 %routed_ffn.1 = bf16[16,384]{1,0:T(8,128)(2,1)} custom-call(bf16[16,6144]{1,0:T(8,128)(2,1)} %tok_hbm.1, s32[2,16]{1,0:T(2,128)} %bitcast.2, s32[2,16]{1,0:T(2,128)} %bitcast.3, bf16[1,3072,4096]{2,1,0:T(8,128)(2,1)} %wg_hbm.1, bf16[1,3072,4096]{2,1,0:T(8,128)(2,1)} %wu_hbm.1, bf16[1,4096,3072]{2,1,0:T(8,128)(2,1)} %wd_hbm.1), custom_call_target="tpu_custom_call" | custom-call | tf_op jit(solution)/shard_map/routed_ffn/pallas_call | solution.py:314
  35.4 1.3 %copy.8 = bf16[16,384]{1,0:T(8,128)(2,1)} copy(bf16[16,384]{1,0:T(8,128)(2,1)} %routed_ffn.1) | data formatting | bytes 24576

commit v2 on v1

v2 whole, which is shorter than its diff:
```python
import functools

import jax
import jax.numpy as jnp
from jax import lax
from jax.experimental import pallas as pl
from jax.experimental.pallas import tpu as pltpu
from jax.sharding import PartitionSpec as P

CAP = 12
LOW = 8
PIECE = 16
ROWS = 24
STEPS = 8
EARLY = 4
RING = 5
LAG = 3
FIRST = 2
MESH = pl.DeviceIdType.MESH
F32, BF16 = jnp.float32, jnp.bfloat16


def plain(tokens, route, weight_q, w_gate, w_up, w_down):
    expert = lax.axis_index("gx")
    width_z = lax.axis_size("gz")
    owners = lax.axis_size("gy")
    hits = (route == expert).astype(jnp.int32)
    routed = jnp.sum(hits, axis=1)
    slot_index = jnp.cumsum(routed) - 1
    columns = jnp.arange(CAP, dtype=jnp.int32)
    placing = (slot_index[None, :] == columns[:, None]) & (routed[None, :] > 0)
    place_half = placing.astype(jnp.bfloat16)
    place_full = placing.astype(jnp.float32)
    outgoing = jnp.dot(place_half, tokens, preferred_element_type=jnp.float32).astype(jnp.bfloat16)
    weights_f = weight_q.astype(jnp.float32)
    shares = weights_f / jnp.sum(weights_f, axis=1, keepdims=True)
    token_gate = jnp.sum(hits.astype(jnp.float32) * shares, axis=1)
    slot_gate = jnp.dot(place_full, token_gate, precision=lax.Precision.HIGHEST)
    depth = w_gate.shape[1]
    half = outgoing.reshape(CAP, owners, depth).transpose(1, 0, 2)
    piece = lax.all_to_all(half, "gy", split_axis=0, concat_axis=0, tiled=True)
    piece = piece.reshape(owners * CAP, depth)
    gate = jnp.dot(piece, w_gate[0], preferred_element_type=jnp.float32)
    upper = jnp.dot(piece, w_up[0], preferred_element_type=jnp.float32)
    both = lax.psum_scatter(jnp.stack([gate, upper]), "gy", scatter_dimension=2, tiled=True)
    hidden = (jax.nn.silu(both[0]) * both[1]).astype(jnp.bfloat16)
    down_local = w_down[0]
    partial_value = jnp.dot(
        lax.all_gather(hidden, "gy", axis=1, tiled=True),
        down_local,
        preferred_element_type=jnp.float32,
    )
    portion = CAP // width_z
    column_width = partial_value.shape[1]
    blocks = partial_value.reshape(owners, width_z, portion, column_width)
    narrowed = lax.psum_scatter(blocks, "gz", scatter_dimension=1, tiled=True)
    arrived = lax.all_to_all(narrowed, "gy", split_axis=0, concat_axis=1, tiled=True)
    full = jnp.transpose(arrived[0], (1, 0, 2)).reshape(portion, owners * column_width)
    first = lax.axis_index("gz") * portion
    gate_part = lax.dynamic_slice_in_dim(slot_gate, first, portion, 0)
    place_part = lax.dynamic_slice_in_dim(place_full, first, portion, 0)
    weighted = gate_part[:, None] * full
    contribution = jnp.dot(place_part.T, weighted, precision=lax.Precision.HIGHEST)
    result = lax.psum_scatter(contribution, ("gx", "gz"), scatter_dimension=1, tiled=True)
    return result.astype(jnp.bfloat16)


def kernel(sizes, tok_hbm, route_hbm, wq_hbm, wg_hbm, wu_hbm, wd_hbm, out_ref,
           tok, route, wq, gbuf, ubuf, dbuf_a, dbuf_b, xb, xsend, xs, part, precv,
           hid, late, acc, sbuf, rbuf, sem_in, sem_g, sem_u, sem_a, sem_b, stage,
           tok_ss, tok_rs, ex_ss, ex_rs, hid_ss, hid_rs, out_ss, out_rs):
    nx, ny, nz = sizes
    gx, gy, gz = lax.axis_index("gx"), lax.axis_index("gy"), lax.axis_index("gz")
    other = 1 - gy
    depth, ffl = wg_hbm.shape[1], wg_hbm.shape[2]
    cn = ffl // STEPS
    hw = cn // ny
    width = wd_hbm.shape[2]
    nb = nx * nz // ny
    bw = width // nb
    token_rows = tok.shape[0]
    kb = EARLY * cn
    partner = (gx, other, gz)

    def pair(j):
        slot = lax.rem(j, RING)
        cols = pl.ds(pl.multiple_of(j * cn, cn), cn)
        return (pltpu.make_async_copy(wg_hbm.at[0, :, cols], gbuf.at[slot], sem_g.at[slot]),
                pltpu.make_async_copy(wu_hbm.at[0, :, cols], ubuf.at[slot], sem_u.at[slot]))

    def down_a(j):
        rows = pl.ds(pl.multiple_of(j * cn, cn), cn)
        return pltpu.make_async_copy(wd_hbm.at[0, rows, :], dbuf_a.at[j], sem_a.at[j])

    per = nb // nz

    def block_of(i):
        z = jnp.where(gz < nz // 2, nz - 1 - i // per, i // per)
        return lax.rem(i, per) * nz + z, lax.rem(i, per), z

    def down_b(i):
        b, _, _ = block_of(i)
        cols = pl.ds(pl.multiple_of(b * bw, 128), bw)
        return pltpu.make_async_copy(wd_hbm.at[0, kb:, cols], dbuf_b.at[i], sem_b.at[i])

    ins = [pltpu.make_async_copy(tok_hbm, tok, sem_in.at[0]),
           pltpu.make_async_copy(route_hbm, route, sem_in.at[1]),
           pltpu.make_async_copy(wq_hbm, wq, sem_in.at[2])]
    for c in ins:
        c.start()
    for j in range(RING):
        for c in pair(j):
            c.start()
    for j in range(FIRST):
        down_a(j).start()

    near_count = (nx - 1) + (ny - 1) + (gz > 0).astype(jnp.int32) + (gz < nz - 1).astype(jnp.int32)

    def signal_near(sem):
        pl.semaphore_signal(sem, inc=1, device_id=partner, device_id_type=MESH)
        for d in range(1, nx):
            pl.semaphore_signal(sem, inc=1, device_id=(lax.rem(gx + d, nx), gy, gz), device_id_type=MESH)

        @pl.when(gz > 0)
        def _():
            pl.semaphore_signal(sem, inc=1, device_id=(gx, gy, gz - 1), device_id_type=MESH)

        @pl.when(gz < nz - 1)
        def _():
            pl.semaphore_signal(sem, inc=1, device_id=(gx, gy, gz + 1), device_id_type=MESH)

    barrier = pltpu.get_barrier_semaphore()
    signal_near(barrier)

    for c in ins:
        c.wait()

    lane_t = lax.broadcasted_iota(jnp.int32, (token_rows, token_rows), 1)
    sub_t = lax.broadcasted_iota(jnp.int32, (token_rows, token_rows), 0)
    eye = (lane_t == sub_t).astype(F32)
    upto = (lane_t <= sub_t).astype(F32)
    since = (sub_t <= lane_t).astype(F32)
    r0, r1 = route[0:1, :], route[1:2, :]
    shift = gy.astype(F32) * (PIECE - CAP)

    def hit_row(e):
        return ((r0 == e) | (r1 == e)).astype(F32)

    def row_of(slot):
        return jnp.where(slot < LOW, slot, slot + shift)

    hr = hit_row(gx)
    hc = jnp.sum(eye * hr, axis=1, keepdims=True)
    slot_row = row_of(jnp.sum(since * hc, axis=0, keepdims=True) - 1.0)
    rows_sub = lax.broadcasted_iota(jnp.int32, (PIECE, token_rows), 0).astype(F32)
    place = ((slot_row == rows_sub) & (hr > 0.0)).astype(F32).astype(BF16)

    thirds = 3
    span = depth // thirds
    for q in range(thirds):
        theirs = pl.ds(pl.multiple_of(other * depth + q * span, 128), span)
        xsend[:, q * span:(q + 1) * span] = jnp.dot(
            place, tok[:, theirs], preferred_element_type=F32).astype(BF16)

    pl.semaphore_wait(barrier, near_count)
    tok_copy = pltpu.make_async_remote_copy(
        src_ref=xsend, dst_ref=xb.at[gy], send_sem=tok_ss, recv_sem=tok_rs,
        device_id=partner, device_id_type=MESH)
    tok_copy.start()
    signal_near(stage.at[0])

    for q in range(thirds):
        ours = pl.ds(pl.multiple_of(gy * depth + q * span, 128), span)
        xb[gy, :, q * span:(q + 1) * span] = jnp.dot(
            place, tok[:, ours], preferred_element_type=F32).astype(BF16)
    acc[...] = jnp.zeros_like(acc)

    w0, w1 = wq[0:1, :].astype(F32), wq[1:2, :].astype(F32)
    total = w0 + w1
    s0, s1 = w0 / total, w1 / total
    spreads = []
    rows_lane = lax.broadcasted_iota(jnp.int32, (token_rows, PIECE), 1).astype(F32)
    for e in range(nx):
        h = hit_row(e)
        g = jnp.where(r0 == e, s0, 0.0) + jnp.where(r1 == e, s1, 0.0)
        slot_col = row_of(jnp.sum(upto * h, axis=1, keepdims=True) - 1.0)
        gate_col = jnp.sum(eye * g, axis=1, keepdims=True)
        hit_col = jnp.sum(eye * h, axis=1, keepdims=True)
        spreads.append(jnp.where((slot_col == rows_lane) & (hit_col > 0.0), gate_col, 0.0))

    tok_copy.wait()
    for q in range(thirds):
        cols = slice(q * span, (q + 1) * span)
        x0, x1 = xb[0, :, cols].astype(F32), xb[1, :, cols].astype(F32)
        xs[:, cols] = jnp.concatenate(
            [x0[:LOW], x1[:LOW], x0[LOW:] + x1[LOW:]], axis=0).astype(BF16)

    def exchange(j):
        return pltpu.make_async_remote_copy(
            src_ref=part.at[j, other], dst_ref=precv.at[j], send_sem=ex_ss.at[j],
            recv_sem=ex_rs.at[j], device_id=partner, device_id_type=MESH)

    def share(j):
        return pltpu.make_async_remote_copy(
            src_ref=hid.at[j, gy], dst_ref=hid.at[j, gy], send_sem=hid_ss.at[j],
            recv_sem=hid_rs.at[j], device_id=partner, device_id_type=MESH)

    def finish(j):
        exchange(j).wait_recv()
        g = part[j, gy, 0] + precv[j, 0]
        u = part[j, gy, 1] + precv[j, 1]
        hid[j, gy] = (g * jax.nn.sigmoid(g) * u).astype(BF16)
        share(j).start()

    def project(j, carry):
        @pl.when(j < nz)
        def _():
            pl.semaphore_wait(stage.at[j], near_count)

        @pl.when(j < nz - 1)
        def _():
            signal_near(stage.at[j + 1])

        slot = lax.rem(j, RING)
        cg, cu = pair(j)
        cg.wait()
        g = jnp.dot(xs[...], gbuf[slot], preferred_element_type=F32)
        for h in range(ny):
            part[j, h, 0] = g[:, h * hw:(h + 1) * hw]
        cu.wait()
        u = jnp.dot(xs[...], ubuf[slot], preferred_element_type=F32)
        for h in range(ny):
            part[j, h, 1] = u[:, h * hw:(h + 1) * hw]
        exchange(j).start()

        @pl.when(j + RING < STEPS)
        def _():
            for c in pair(j + RING):
                c.start()

        @pl.when(j + RING == STEPS - 1)
        def _():
            for t in range(FIRST, EARLY):
                down_a(t).start()
            for t in range(nb):
                down_b(t).start()

        @pl.when(j >= LAG)
        def _():
            finish(j - LAG)
        return carry

    lax.fori_loop(0, STEPS, project, 0)

    nsub = 4
    sw = width // nsub

    def first_part(j, carry):
        @pl.when(j < LAG)
        def _():
            finish(STEPS - LAG + j)

        share(j).wait_recv()
        down_a(j).wait()
        for q in range(nsub):
            cols = slice(q * sw, (q + 1) * sw)
            y = acc[:, cols]
            for h in range(ny):
                y = y + jnp.dot(hid[j, h], dbuf_a[j, h * hw:(h + 1) * hw, cols],
                                preferred_element_type=F32)
            acc[:, cols] = y
        return carry

    lax.fori_loop(0, EARLY, first_part, 0)
    for j in range(EARLY, STEPS):
        share(j).wait_recv()
        for h in range(ny):
            start = (j - EARLY) * cn + h * hw
            late[:, start:start + hw] = hid[j, h]

    def out_copy(i, o):
        _, c, z = block_of(i)
        here = gx * nz + gz
        return pltpu.make_async_remote_copy(
            src_ref=sbuf.at[i, o], dst_ref=rbuf.at[here], send_sem=out_ss.at[i, o],
            recv_sem=out_rs.at[here], device_id=(gy * per + c, o, z), device_id_type=MESH)

    def to_self(i, o):
        _, c, z = block_of(i)
        return (gy * per + c == gx) & (o == gy) & (z == gz)

    def second_part(i, carry):
        b, c, z = block_of(i)
        cols = pl.ds(pl.multiple_of(b * bw, 128), bw)
        down_b(i).wait()
        y = acc[:, cols] + jnp.dot(late[...], dbuf_b[i], preferred_element_type=F32)
        for o in range(ny):
            sent = jnp.concatenate([y[o * LOW:(o + 1) * LOW], y[ny * LOW:]], axis=0).astype(BF16)
            sbuf[i, o] = sent

            @pl.when(to_self(i, o))
            def _():
                rbuf[gx * nz + gz] = sent

            @pl.when(jnp.logical_not(to_self(i, o)))
            def _():
                out_copy(i, o).start()
        return carry

    lax.fori_loop(0, nb, second_part, 0)

    src_y = (gx * nz + gz) // nb
    for e in range(nx):
        for z in range(nz):
            @pl.when(jnp.logical_not((e == gx) & (src_y == gy) & (z == gz)))
            def _():
                pltpu.make_async_remote_copy(
                    src_ref=sbuf.at[0, 0], dst_ref=rbuf.at[e * nz + z], send_sem=out_ss.at[0, 0],
                    recv_sem=out_rs.at[e * nz + z], device_id=(e, src_y, z),
                    device_id_type=MESH).wait_recv()
    sums = []
    for e in range(nx):
        s = rbuf[e * nz].astype(F32)
        for z in range(1, nz):
            s = s + rbuf[e * nz + z].astype(F32)
        sums.append(jnp.dot(spreads[e], s, precision=lax.Precision.HIGHEST,
                            preferred_element_type=F32))
    out_ref[...] = functools.reduce(lambda a, b: a + b, sums).astype(out_ref.dtype)

    def drain(j, carry):
        exchange(j).wait_send()
        share(j).wait_send()
        return carry

    lax.fori_loop(0, STEPS, drain, 0)

    def drain_out(i, carry):
        for o in range(ny):
            @pl.when(jnp.logical_not(to_self(i, o)))
            def _():
                out_copy(i, o).wait_send()
        return carry

    lax.fori_loop(0, nb, drain_out, 0)


def fused(sizes, tokens, route, weight_q, w_gate, w_up, w_down):
    nx, ny, nz = sizes
    depth, ffl = w_gate.shape[1], w_gate.shape[2]
    width = w_down.shape[2]
    cn = ffl // STEPS
    hw = cn // ny
    nb = nx * nz // ny
    bw = width // nb
    rest = ffl - EARLY * cn
    dma = pltpu.SemaphoreType.DMA
    hbm = pl.BlockSpec(memory_space=pl.ANY)
    return pl.pallas_call(
        functools.partial(kernel, sizes),
        out_shape=jax.ShapeDtypeStruct((tokens.shape[0], bw), BF16),
        in_specs=[hbm] * 6,
        out_specs=pl.BlockSpec(memory_space=pltpu.VMEM),
        scratch_shapes=[
            pltpu.VMEM(tokens.shape, BF16),
            pltpu.VMEM(route.shape[::-1], jnp.int32),
            pltpu.VMEM(route.shape[::-1], jnp.int32),
            pltpu.VMEM((RING, depth, cn), BF16),
            pltpu.VMEM((RING, depth, cn), BF16),
            pltpu.VMEM((EARLY, cn, width), BF16),
            pltpu.VMEM((nb, rest, bw), BF16),
            pltpu.VMEM((ny, PIECE, depth), BF16),
            pltpu.VMEM((PIECE, depth), BF16),
            pltpu.VMEM((ROWS, depth), BF16),
            pltpu.VMEM((STEPS, ny, 2, ROWS, hw), F32),
            pltpu.VMEM((STEPS, 2, ROWS, hw), F32),
            pltpu.VMEM((STEPS, ny, ROWS, hw), BF16),
            pltpu.VMEM((ROWS, rest), BF16),
            pltpu.VMEM((ROWS, width), F32),
            pltpu.VMEM((nb, ny, PIECE, bw), BF16),
            pltpu.VMEM((nx * nz, PIECE, bw), BF16),
            dma((3,)), dma((RING,)), dma((RING,)), dma((EARLY,)), dma((nb,)),
            pltpu.SemaphoreType.REGULAR((nz,)),
            dma, dma, dma((STEPS,)), dma((STEPS,)), dma((STEPS,)), dma((STEPS,)),
            dma((nb, ny)), dma((nx * nz,)),
        ],
        compiler_params=pltpu.CompilerParams(
            collective_id=0, has_side_effects=True, vmem_limit_bytes=67043328),
        name="routed_ffn",
    )(tokens, route.T, weight_q.T, w_gate, w_up, w_down)


def solution(mesh):
    in_specs = (
        P("gy", None),
        P("gy", None),
        P("gy", None),
        P("gx", "gy", "gz"),
        P("gx", "gy", "gz"),
        P("gx", "gz", "gy"),
    )
    out_specs = P("gy", ("gx", "gz"))
    sizes = tuple(mesh.shape[name] for name in ("gx", "gy", "gz"))
    body = functools.partial(fused, sizes) if sizes[1] == 2 else plain
    return jax.shard_map(
        body, mesh=mesh, in_specs=in_specs, out_specs=out_specs, check_vma=False
    )
```

time: 36.9 us -> 44.1 us (1.20)
  Pallas kernels: 35.4 us -> 42.6 us
    pallas_call x1, Pallas kernels: 35.4 us -> 42.6 us  [fused(): pl.pallas_call(functools.partial(kernel, sizes), out_shape=jax.ShapeDtype...]
where the time goes in v2:
time: 44.1 us; the launch traced here: 43.9 us
  Pallas kernels  42.6 us (97%)
  local copies, waits for them, and re-layouts  1.31 us (3%)
    pallas_call x1, Pallas kernels, fused(): pl.pallas_call(functools.partial(kernel, sizes), out_shape=jax.ShapeDtype...  42.6 us
    unnamed x1, local copies, waits for them, and re-layouts  1.31 us

profile of v2, /device:TPU:0, one launch (start us, length us, event | category | flops | bytes accessed | tf_op | source)
XLA Modules:
  0.0 43.9 jit_solution(3199135618447760145)
XLA Ops:
  0.0 42.6 %routed_ffn.1 = bf16[16,384]{1,0:T(8,128)(2,1)} custom-call(bf16[16,6144]{1,0:T(8,128)(2,1)} %tok_hbm.1, s32[2,16]{1,0:T(2,128)} %bitcast.2, s32[2,16]{1,0:T(2,128)} %bitcast.3, bf16[1,3072,4096]{2,1,0:T(8,128)(2,1)} %wg_hbm.1, bf16[1,3072,4096]{2,1,0:T(8,128)(2,1)} %wu_hbm.1, bf16[1,4096,3072]{2,1,0:T(8,128)(2,1)} %wd_hbm.1), custom_call_target="tpu_custom_call" | custom-call | tf_op jit(solution)/shard_map/routed_ffn/pallas_call | solution.py:358
  42.6 1.3 %copy.8 = bf16[16,384]{1,0:T(8,128)(2,1)} copy(bf16[16,384]{1,0:T(8,128)(2,1)} %routed_ffn.1) | data formatting | bytes 24576

commit v3 on v2

--- a/solution.py
+++ b/solution.py
@@ -12,10 +12,9 @@
 PIECE = 16
 ROWS = 24
 STEPS = 8
-EARLY = 4
+EARLY = 6
 RING = 5
 LAG = 3
-FIRST = 2
 MESH = pl.DeviceIdType.MESH
 F32, BF16 = jnp.float32, jnp.bfloat16
 
@@ -101,26 +100,23 @@
     def down_b(i):
         b, _, _ = block_of(i)
         cols = pl.ds(pl.multiple_of(b * bw, 128), bw)
-        return pltpu.make_async_copy(wd_hbm.at[0, kb:, cols], dbuf_b.at[i], sem_b.at[i])
+        return pltpu.make_async_copy(
+            wd_hbm.at[0, kb:, cols],
+            dbuf_b.at[i // per, :, pl.ds(pl.multiple_of(lax.rem(i, per) * bw, 128), bw)],
+            sem_b.at[i])
 
     ins = [pltpu.make_async_copy(tok_hbm, tok, sem_in.at[0]),
            pltpu.make_async_copy(route_hbm, route, sem_in.at[1]),
            pltpu.make_async_copy(wq_hbm, wq, sem_in.at[2])]
     for c in ins:
         c.start()
-    for j in range(RING):
+    for j in range(1):
         for c in pair(j):
             c.start()
-    for j in range(FIRST):
-        down_a(j).start()
-
-    near_count = (nx - 1) + (ny - 1) + (gz > 0).astype(jnp.int32) + (gz < nz - 1).astype(jnp.int32)
-
-    def signal_near(sem):
-        pl.semaphore_signal(sem, inc=1, device_id=partner, device_id_type=MESH)
-        for d in range(1, nx):
-            pl.semaphore_signal(sem, inc=1, device_id=(lax.rem(gx + d, nx), gy, gz), device_id_type=MESH)
-
+
+    line_count = (gz > 0).astype(jnp.int32) + (gz < nz - 1).astype(jnp.int32)
+
+    def signal_line(sem):
         @pl.when(gz > 0)
         def _():
             pl.semaphore_signal(sem, inc=1, device_id=(gx, gy, gz - 1), device_id_type=MESH)
@@ -130,10 +126,16 @@
             pl.semaphore_signal(sem, inc=1, device_id=(gx, gy, gz + 1), device_id_type=MESH)
 
     barrier = pltpu.get_barrier_semaphore()
-    signal_near(barrier)
+    pl.semaphore_signal(barrier, inc=1, device_id=partner, device_id_type=MESH)
+    for d in range(1, nx):
+        pl.semaphore_signal(barrier, inc=1, device_id=(lax.rem(gx + d, nx), gy, gz), device_id_type=MESH)
+    signal_line(barrier)
 
     for c in ins:
         c.wait()
+    for j in range(1, RING):
+        for c in pair(j):
+            c.start()
 
     lane_t = lax.broadcasted_iota(jnp.int32, (token_rows, token_rows), 1)
     sub_t = lax.broadcasted_iota(jnp.int32, (token_rows, token_rows), 0)
@@ -159,20 +161,19 @@
     span = depth // thirds
     for q in range(thirds):
         theirs = pl.ds(pl.multiple_of(other * depth + q * span, 128), span)
-        xsend[:, q * span:(q + 1) * span] = jnp.dot(
-            place, tok[:, theirs], preferred_element_type=F32).astype(BF16)
-
-    pl.semaphore_wait(barrier, near_count)
-    tok_copy = pltpu.make_async_remote_copy(
-        src_ref=xsend, dst_ref=xb.at[gy], send_sem=tok_ss, recv_sem=tok_rs,
-        device_id=partner, device_id_type=MESH)
-    tok_copy.start()
-    signal_near(stage.at[0])
+        xsend[q] = jnp.dot(place, tok[:, theirs], preferred_element_type=F32).astype(BF16)
+
+    pl.semaphore_wait(barrier, (nx - 1) + (ny - 1) + line_count)
+    tok_copies = [pltpu.make_async_remote_copy(
+        src_ref=xsend.at[q], dst_ref=xb.at[gy, q], send_sem=tok_ss.at[q], recv_sem=tok_rs.at[q],
+        device_id=partner, device_id_type=MESH) for q in range(thirds)]
+    for c in tok_copies:
+        c.start()
+    pl.semaphore_signal(stage.at[0], inc=1, device_id=partner, device_id_type=MESH)
 
     for q in range(thirds):
         ours = pl.ds(pl.multiple_of(gy * depth + q * span, 128), span)
-        xb[gy, :, q * span:(q + 1) * span] = jnp.dot(
-            place, tok[:, ours], preferred_element_type=F32).astype(BF16)
+        xb[gy, q] = jnp.dot(place, tok[:, ours], preferred_element_type=F32).astype(BF16)
     acc[...] = jnp.zeros_like(acc)
 
     w0, w1 = wq[0:1, :].astype(F32), wq[1:2, :].astype(F32)
@@ -188,13 +189,6 @@
         hit_col = jnp.sum(eye * h, axis=1, keepdims=True)
         spreads.append(jnp.where((slot_col == rows_lane) & (hit_col > 0.0), gate_col, 0.0))
 
-    tok_copy.wait()
-    for q in range(thirds):
-        cols = slice(q * span, (q + 1) * span)
-        x0, x1 = xb[0, :, cols].astype(F32), xb[1, :, cols].astype(F32)
-        xs[:, cols] = jnp.concatenate(
-            [x0[:LOW], x1[:LOW], x0[LOW:] + x1[LOW:]], axis=0).astype(BF16)
-
     def exchange(j):
         return pltpu.make_async_remote_copy(
             src_ref=part.at[j, other], dst_ref=precv.at[j], send_sem=ex_ss.at[j],
@@ -212,54 +206,75 @@
         hid[j, gy] = (g * jax.nn.sigmoid(g) * u).astype(BF16)
         share(j).start()
 
-    def project(j, carry):
-        @pl.when(j < nz)
-        def _():
-            pl.semaphore_wait(stage.at[j], near_count)
-
-        @pl.when(j < nz - 1)
-        def _():
-            signal_near(stage.at[j + 1])
-
-        slot = lax.rem(j, RING)
-        cg, cu = pair(j)
-        cg.wait()
-        g = jnp.dot(xs[...], gbuf[slot], preferred_element_type=F32)
+    def fetch_next(j):
+        @pl.when(j + RING < STEPS)
+        def _():
+            for c in pair(j + RING):
+                c.start()
+
+        t = j + RING - STEPS
+
+        @pl.when((t >= 0) & (t < EARLY // 2))
+        def _():
+            down_a(2 * t).start()
+            down_a(2 * t + 1).start()
+
+        @pl.when(t == EARLY // 2)
+        def _():
+            for i in range(nb):
+                down_b(i).start()
+
+    def hand_over(j, g, u):
         for h in range(ny):
             part[j, h, 0] = g[:, h * hw:(h + 1) * hw]
-        cu.wait()
-        u = jnp.dot(xs[...], ubuf[slot], preferred_element_type=F32)
-        for h in range(ny):
             part[j, h, 1] = u[:, h * hw:(h + 1) * hw]
         exchange(j).start()
-
-        @pl.when(j + RING < STEPS)
-        def _():
-            for c in pair(j + RING):
-                c.start()
-
-        @pl.when(j + RING == STEPS - 1)
-        def _():
-            for t in range(FIRST, EARLY):
-                down_a(t).start()
-            for t in range(nb):
-                down_b(t).start()
+        fetch_next(j)
+
+    for c in pair(0):
+        c.wait()
+    g = u = jnp.zeros((ROWS, cn), F32)
+    for q in range(thirds):
+        cols = slice(q * span, (q + 1) * span)
+        tok_copies[q].wait()
+        x0, x1 = xb[0, q].astype(F32), xb[1, q].astype(F32)
+        x = jnp.concatenate([x0[:LOW], x1[:LOW], x0[LOW:] + x1[LOW:]], axis=0).astype(BF16)
+        xs[:, cols] = x
+        g = g + jnp.dot(x, gbuf[0, cols, :], preferred_element_type=F32)
+        u = u + jnp.dot(x, ubuf[0, cols, :], preferred_element_type=F32)
+    hand_over(0, g, u)
+
+    def project(j, carry):
+        @pl.when(j == 1)
+        def _():
+            pl.semaphore_wait(stage.at[0], ny - 1)
+
+        @pl.when((j > 1) & (j <= nz))
+        def _():
+            pl.semaphore_wait(stage.at[j - 1], line_count)
+
+        @pl.when(j < nz)
+        def _():
+            signal_line(stage.at[j])
+
+        for c in pair(j):
+            c.wait()
+        slot = lax.rem(j, RING)
+        g = jnp.dot(xs[...], gbuf[slot], preferred_element_type=F32)
+        u = jnp.dot(xs[...], ubuf[slot], preferred_element_type=F32)
+        hand_over(j, g, u)
 
         @pl.when(j >= LAG)
         def _():
             finish(j - LAG)
         return carry
 
-    lax.fori_loop(0, STEPS, project, 0)
+    lax.fori_loop(1, STEPS, project, 0)
 
     nsub = 4
     sw = width // nsub
 
     def first_part(j, carry):
-        @pl.when(j < LAG)
-        def _():
-            finish(STEPS - LAG + j)
-
         share(j).wait_recv()
         down_a(j).wait()
         for q in range(nsub):
@@ -269,6 +284,10 @@
                 y = y + jnp.dot(hid[j, h], dbuf_a[j, h * hw:(h + 1) * hw, cols],
                                 preferred_element_type=F32)
             acc[:, cols] = y
+
+        @pl.when(j < LAG)
+        def _():
+            finish(STEPS - LAG + j)
         return carry
 
     lax.fori_loop(0, EARLY, first_part, 0)
@@ -289,25 +308,28 @@
         _, c, z = block_of(i)
         return (gy * per + c == gx) & (o == gy) & (z == gz)
 
-    def second_part(i, carry):
-        b, c, z = block_of(i)
-        cols = pl.ds(pl.multiple_of(b * bw, 128), bw)
-        down_b(i).wait()
-        y = acc[:, cols] + jnp.dot(late[...], dbuf_b[i], preferred_element_type=F32)
-        for o in range(ny):
-            sent = jnp.concatenate([y[o * LOW:(o + 1) * LOW], y[ny * LOW:]], axis=0).astype(BF16)
-            sbuf[i, o] = sent
-
-            @pl.when(to_self(i, o))
-            def _():
-                rbuf[gx * nz + gz] = sent
-
-            @pl.when(jnp.logical_not(to_self(i, o)))
-            def _():
-                out_copy(i, o).start()
+    def second_part(k, carry):
+        for c in range(per):
+            down_b(k * per + c).wait()
+        y = jnp.dot(late[...], dbuf_b[k], preferred_element_type=F32)
+        for c in range(per):
+            i = k * per + c
+            b, _, _ = block_of(i)
+            yc = acc[:, pl.ds(pl.multiple_of(b * bw, 128), bw)] + y[:, c * bw:(c + 1) * bw]
+            for o in range(ny):
+                sent = jnp.concatenate([yc[o * LOW:(o + 1) * LOW], yc[ny * LOW:]], axis=0).astype(BF16)
+                sbuf[i, o] = sent
+
+                @pl.when(to_self(i, o))
+                def _():
+                    rbuf[gx * nz + gz] = sent
+
+                @pl.when(jnp.logical_not(to_self(i, o)))
+                def _():
+                    out_copy(i, o).start()
         return carry
 
-    lax.fori_loop(0, nb, second_part, 0)
+    lax.fori_loop(0, nz, second_part, 0)
 
     src_y = (gx * nz + gz) // nb
     for e in range(nx):
@@ -367,9 +389,9 @@
             pltpu.VMEM((RING, depth, cn), BF16),
             pltpu.VMEM((RING, depth, cn), BF16),
             pltpu.VMEM((EARLY, cn, width), BF16),
-            pltpu.VMEM((nb, rest, bw), BF16),
-            pltpu.VMEM((ny, PIECE, depth), BF16),
-            pltpu.VMEM((PIECE, depth), BF16),
+            pltpu.VMEM((nz, rest, nb // nz * bw), BF16),
+            pltpu.VMEM((ny, 3, PIECE, depth // 3), BF16),
+            pltpu.VMEM((3, PIECE, depth // 3), BF16),
             pltpu.VMEM((ROWS, depth), BF16),
             pltpu.VMEM((STEPS, ny, 2, ROWS, hw), F32),
             pltpu.VMEM((STEPS, 2, ROWS, hw), F32),
@@ -380,7 +402,7 @@
             pltpu.VMEM((nx * nz, PIECE, bw), BF16),
             dma((3,)), dma((RING,)), dma((RING,)), dma((EARLY,)), dma((nb,)),
             pltpu.SemaphoreType.REGULAR((nz,)),
-            dma, dma, dma((STEPS,)), dma((STEPS,)), dma((STEPS,)), dma((STEPS,)),
+            dma((3,)), dma((3,)), dma((STEPS,)), dma((STEPS,)), dma((STEPS,)), dma((STEPS,)),
             dma((nb, ny)), dma((nx * nz,)),
         ],
         compiler_params=pltpu.CompilerParams(

time: 44.1 us -> 34.6 us (0.78)
  Pallas kernels: 42.6 us -> 33.1 us
    pallas_call x1, Pallas kernels: 42.6 us -> 33.1 us  [fused(): pl.pallas_call(functools.partial(kernel, sizes), out_shape=jax.ShapeDtype...]
where the time goes in v3:
time: 34.6 us; the launch traced here: 34.4 us
  Pallas kernels  33.1 us (96%)
  local copies, waits for them, and re-layouts  1.31 us (4%)
    pallas_call x1, Pallas kernels, fused(): pl.pallas_call(functools.partial(kernel, sizes), out_shape=jax.ShapeDtype...  33.1 us
    unnamed x1, local copies, waits for them, and re-layouts  1.31 us

profile of v3, /device:TPU:0, one launch (start us, length us, event | category | flops | bytes accessed | tf_op | source)
XLA Modules:
  0.0 34.4 jit_solution(15875731322864760148)
XLA Ops:
  0.0 33.1 %routed_ffn.1 = bf16[16,384]{1,0:T(8,128)(2,1)} custom-call(bf16[16,6144]{1,0:T(8,128)(2,1)} %tok_hbm.1, s32[2,16]{1,0:T(2,128)} %bitcast.2, s32[2,16]{1,0:T(2,128)} %bitcast.3, bf16[1,3072,4096]{2,1,0:T(8,128)(2,1)} %wg_hbm.1, bf16[1,3072,4096]{2,1,0:T(8,128)(2,1)} %wu_hbm.1, bf16[1,4096,3072]{2,1,0:T(8,128)(2,1)} %wd_hbm.1), custom_call_target="tpu_custom_call" | custom-call | tf_op jit(solution)/shard_map/routed_ffn/pallas_call | solution.py:380
  33.1 1.3 %copy.8 = bf16[16,384]{1,0:T(8,128)(2,1)} copy(bf16[16,384]{1,0:T(8,128)(2,1)} %routed_ffn.1) | data formatting | bytes 24576

commit v4 on v3

--- a/solution.py
+++ b/solution.py
@@ -12,7 +12,8 @@
 PIECE = 16
 ROWS = 24
 STEPS = 8
-EARLY = 6
+EARLY = 4
+DIRECT = 2
 RING = 5
 LAG = 3
 MESH = pl.DeviceIdType.MESH
@@ -66,8 +67,8 @@
 
 def kernel(sizes, tok_hbm, route_hbm, wq_hbm, wg_hbm, wu_hbm, wd_hbm, out_ref,
            tok, route, wq, gbuf, ubuf, dbuf_a, dbuf_b, xb, xsend, xs, part, precv,
-           hid, late, acc, sbuf, rbuf, sem_in, sem_g, sem_u, sem_a, sem_b, stage,
-           tok_ss, tok_rs, ex_ss, ex_rs, hid_ss, hid_rs, out_ss, out_rs):
+           whole, wrecv, hid, late, acc, sbuf, rbuf, sem_in, sem_g, sem_u, sem_a, sem_b, stage,
+           tok_ss, tok_rs, cr_ss, cr_rs, ex_ss, ex_rs, hid_ss, hid_rs, out_ss, out_rs):
     nx, ny, nz = sizes
     gx, gy, gz = lax.axis_index("gx"), lax.axis_index("gy"), lax.axis_index("gz")
     other = 1 - gy
@@ -212,24 +213,23 @@
             for c in pair(j + RING):
                 c.start()
 
-        t = j + RING - STEPS
-
-        @pl.when((t >= 0) & (t < EARLY // 2))
-        def _():
-            down_a(2 * t).start()
-            down_a(2 * t + 1).start()
-
-        @pl.when(t == EARLY // 2)
-        def _():
-            for i in range(nb):
-                down_b(i).start()
+        @pl.when(j == STEPS - RING + 1)
+        def _():
+            for t in range(EARLY - 2):
+                down_a(t).start()
+
+        @pl.when(j == STEPS - RING + 2)
+        def _():
+            down_a(EARLY - 2).start()
+
+        @pl.when(j == STEPS - RING + 3)
+        def _():
+            down_a(EARLY - 1).start()
 
     def hand_over(j, g, u):
         for h in range(ny):
             part[j, h, 0] = g[:, h * hw:(h + 1) * hw]
             part[j, h, 1] = u[:, h * hw:(h + 1) * hw]
-        exchange(j).start()
-        fetch_next(j)
 
     for c in pair(0):
         c.wait()
@@ -243,38 +243,69 @@
         g = g + jnp.dot(x, gbuf[0, cols, :], preferred_element_type=F32)
         u = u + jnp.dot(x, ubuf[0, cols, :], preferred_element_type=F32)
     hand_over(0, g, u)
-
-    def project(j, carry):
-        @pl.when(j == 1)
-        def _():
-            pl.semaphore_wait(stage.at[0], ny - 1)
-
-        @pl.when((j > 1) & (j <= nz))
-        def _():
-            pl.semaphore_wait(stage.at[j - 1], line_count)
-
-        @pl.when(j < nz)
-        def _():
-            signal_line(stage.at[j])
-
+    exchange(0).start()
+    fetch_next(0)
+
+    def multiply(j):
         for c in pair(j):
             c.wait()
         slot = lax.rem(j, RING)
         g = jnp.dot(xs[...], gbuf[slot], preferred_element_type=F32)
         u = jnp.dot(xs[...], ubuf[slot], preferred_element_type=F32)
         hand_over(j, g, u)
+        return g, u
+
+    def cross(d):
+        return pltpu.make_async_remote_copy(
+            src_ref=whole.at[d], dst_ref=wrecv.at[d], send_sem=cr_ss.at[d],
+            recv_sem=cr_rs.at[d], device_id=partner, device_id_type=MESH)
+
+    def project(j, carry):
+        @pl.when(j == 1)
+        def _():
+            pl.semaphore_wait(stage.at[0], ny - 1)
+
+        @pl.when((j > 1) & (j <= nz))
+        def _():
+            pl.semaphore_wait(stage.at[j - 1], line_count)
+
+        @pl.when(j < nz)
+        def _():
+            signal_line(stage.at[j])
+
+        multiply(j)
+        exchange(j).start()
+        fetch_next(j)
 
         @pl.when(j >= LAG)
         def _():
             finish(j - LAG)
         return carry
 
-    lax.fori_loop(1, STEPS, project, 0)
+    def project_last(j, carry):
+        g, u = multiply(j)
+        d = j - (STEPS - DIRECT)
+        whole[d] = jnp.concatenate([g, u], axis=0).astype(BF16)
+        cross(d).start()
+        fetch_next(j)
+        finish(j - LAG)
+        return carry
+
+    lax.fori_loop(1, STEPS - DIRECT, project, 0)
+    lax.fori_loop(STEPS - DIRECT, STEPS, project_last, 0)
 
     nsub = 4
     sw = width // nsub
 
+    def fetch_blocks(k):
+        for c in range(per):
+            down_b(k * per + c).start()
+
     def first_part(j, carry):
+        @pl.when(j < nz)
+        def _():
+            fetch_blocks(j)
+
         share(j).wait_recv()
         down_a(j).wait()
         for q in range(nsub):
@@ -285,17 +316,29 @@
                                 preferred_element_type=F32)
             acc[:, cols] = y
 
-        @pl.when(j < LAG)
+        @pl.when(j < LAG - DIRECT)
         def _():
             finish(STEPS - LAG + j)
         return carry
 
     lax.fori_loop(0, EARLY, first_part, 0)
+    for k in range(EARLY, nz):
+        fetch_blocks(k)
     for j in range(EARLY, STEPS):
-        share(j).wait_recv()
+        d = j - (STEPS - DIRECT)
+        if d < 0:
+            share(j).wait_recv()
+        else:
+            cross(d).wait_recv()
         for h in range(ny):
             start = (j - EARLY) * cn + h * hw
-            late[:, start:start + hw] = hid[j, h]
+            if d < 0:
+                late[:, start:start + hw] = hid[j, h]
+            else:
+                theirs = wrecv[d, :, h * hw:(h + 1) * hw].astype(F32)
+                g = part[j, h, 0] + theirs[:ROWS]
+                u = part[j, h, 1] + theirs[ROWS:]
+                late[:, start:start + hw] = (g * jax.nn.sigmoid(g) * u).astype(BF16)
 
     def out_copy(i, o):
         _, c, z = block_of(i)
@@ -354,7 +397,9 @@
         share(j).wait_send()
         return carry
 
-    lax.fori_loop(0, STEPS, drain, 0)
+    lax.fori_loop(0, STEPS - DIRECT, drain, 0)
+    for d in range(DIRECT):
+        cross(d).wait_send()
 
     def drain_out(i, carry):
         for o in range(ny):
@@ -394,15 +439,18 @@
             pltpu.VMEM((3, PIECE, depth // 3), BF16),
             pltpu.VMEM((ROWS, depth), BF16),
             pltpu.VMEM((STEPS, ny, 2, ROWS, hw), F32),
-            pltpu.VMEM((STEPS, 2, ROWS, hw), F32),
-            pltpu.VMEM((STEPS, ny, ROWS, hw), BF16),
+            pltpu.VMEM((STEPS - DIRECT, 2, ROWS, hw), F32),
+            pltpu.VMEM((DIRECT, 2 * ROWS, cn), BF16),
+            pltpu.VMEM((DIRECT, 2 * ROWS, cn), BF16),
+            pltpu.VMEM((STEPS - DIRECT, ny, ROWS, hw), BF16),
             pltpu.VMEM((ROWS, rest), BF16),
             pltpu.VMEM((ROWS, width), F32),
             pltpu.VMEM((nb, ny, PIECE, bw), BF16),
             pltpu.VMEM((nx * nz, PIECE, bw), BF16),
             dma((3,)), dma((RING,)), dma((RING,)), dma((EARLY,)), dma((nb,)),
             pltpu.SemaphoreType.REGULAR((nz,)),
-            dma((3,)), dma((3,)), dma((STEPS,)), dma((STEPS,)), dma((STEPS,)), dma((STEPS,)),
+            dma((3,)), dma((3,)), dma((DIRECT,)), dma((DIRECT,)),
+            *[dma((STEPS - DIRECT,))] * 4,
             dma((nb, ny)), dma((nx * nz,)),
         ],
         compiler_params=pltpu.CompilerParams(

time: 34.6 us -> 33.5 us (0.968)
  Pallas kernels: 33.1 us -> 32 us
    pallas_call x1, Pallas kernels: 33.1 us -> 32 us  [fused(): pl.pallas_call(functools.partial(kernel, sizes), out_shape=jax.ShapeDtype...]
where the time goes in v4:
time: 33.5 us; the launch traced here: 33.3 us
  Pallas kernels  32 us (96%)
  local copies, waits for them, and re-layouts  1.31 us (4%)
    pallas_call x1, Pallas kernels, fused(): pl.pallas_call(functools.partial(kernel, sizes), out_shape=jax.ShapeDtype...  32 us
    unnamed x1, local copies, waits for them, and re-layouts  1.31 us

profile of v4, /device:TPU:0, one launch (start us, length us, event | category | flops | bytes accessed | tf_op | source)
XLA Modules:
  0.0 33.3 jit_solution(8097855299752364526)
XLA Ops:
  0.0 32.0 %routed_ffn.1 = bf16[16,384]{1,0:T(8,128)(2,1)} custom-call(bf16[16,6144]{1,0:T(8,128)(2,1)} %tok_hbm.1, s32[2,16]{1,0:T(2,128)} %bitcast.2, s32[2,16]{1,0:T(2,128)} %bitcast.3, bf16[1,3072,4096]{2,1,0:T(8,128)(2,1)} %wg_hbm.1, bf16[1,3072,4096]{2,1,0:T(8,128)(2,1)} %wu_hbm.1, bf16[1,4096,3072]{2,1,0:T(8,128)(2,1)} %wd_hbm.1), custom_call_target="tpu_custom_call" | custom-call | tf_op jit(solution)/shard_map/routed_ffn/pallas_call | solution.py:425
  32.0 1.3 %copy.8 = bf16[16,384]{1,0:T(8,128)(2,1)} copy(bf16[16,384]{1,0:T(8,128)(2,1)} %routed_ffn.1) | data formatting | bytes 24576

commit v5 on v4

--- a/solution.py
+++ b/solution.py
@@ -15,7 +15,7 @@
 EARLY = 4
 DIRECT = 2
 RING = 5
-LAG = 3
+LAG = 2
 MESH = pl.DeviceIdType.MESH
 F32, BF16 = jnp.float32, jnp.bfloat16
 
@@ -375,6 +375,7 @@
     lax.fori_loop(0, nz, second_part, 0)
 
     src_y = (gx * nz + gz) // nb
+    sums = []
     for e in range(nx):
         for z in range(nz):
             @pl.when(jnp.logical_not((e == gx) & (src_y == gy) & (z == gz)))
@@ -383,8 +384,6 @@
                     src_ref=sbuf.at[0, 0], dst_ref=rbuf.at[e * nz + z], send_sem=out_ss.at[0, 0],
                     recv_sem=out_rs.at[e * nz + z], device_id=(e, src_y, z),
                     device_id_type=MESH).wait_recv()
-    sums = []
-    for e in range(nx):
         s = rbuf[e * nz].astype(F32)
         for z in range(1, nz):
             s = s + rbuf[e * nz + z].astype(F32)

time: 33.5 us -> 33.4 us (level)
  no operation moved by 1% of the time
where the time goes in v5:
time: 33.4 us; the launch traced here: 33.2 us
  Pallas kernels  31.9 us (96%)
  local copies, waits for them, and re-layouts  1.31 us (4%)
    pallas_call x1, Pallas kernels, fused(): pl.pallas_call(functools.partial(kernel, sizes), out_shape=jax.ShapeDtype...  31.9 us
    unnamed x1, local copies, waits for them, and re-layouts  1.31 us

profile of v5, /device:TPU:0, one launch (start us, length us, event | category | flops | bytes accessed | tf_op | source)
XLA Modules:
  0.0 33.2 jit_solution(6767326377161395814)
XLA Ops:
  0.0 31.9 %routed_ffn.1 = bf16[16,384]{1,0:T(8,128)(2,1)} custom-call(bf16[16,6144]{1,0:T(8,128)(2,1)} %tok_hbm.1, s32[2,16]{1,0:T(2,128)} %bitcast.2, s32[2,16]{1,0:T(2,128)} %bitcast.3, bf16[1,3072,4096]{2,1,0:T(8,128)(2,1)} %wg_hbm.1, bf16[1,3072,4096]{2,1,0:T(8,128)(2,1)} %wu_hbm.1, bf16[1,4096,3072]{2,1,0:T(8,128)(2,1)} %wd_hbm.1), custom_call_target="tpu_custom_call" | custom-call | tf_op jit(solution)/shard_map/routed_ffn/pallas_call | solution.py:424
  31.9 1.3 %copy.8 = bf16[16,384]{1,0:T(8,128)(2,1)} copy(bf16[16,384]{1,0:T(8,128)(2,1)} %routed_ffn.1) | data formatting | bytes 24576
